TPU v7x, 512 devices: a whole 4x8x8 slice. The times are simulated.
512 devices in a mesh: expert: 8 (over x, core), dp: 64 (over z, y).
Axes of the slice: x: 4, y: 8, z: 8, core: 2. Of those that a mesh axis runs over, the one named last changes fastest.
Arguments:
- tokens: bfloat16 [4096, 4096], P(('expert', 'dp')), may hold values from -6 to 6
- expert_ids: int32 [4096, 2], P(('expert', 'dp')), may hold values from 0 to 7, as said below
- slots: int32 [4096, 2], P(('expert', 'dp')), may hold values from -1 to 1, as said below
- mix_weights: float32 [4096, 2], P(('expert', 'dp')), may hold values from 0.1 to 1
- w_gate: bfloat16 [8, 4096, 8192], P('expert', None, 'dp'), may hold values from -0.09375 to 0.09375
- w_up: bfloat16 [8, 4096, 8192], P('expert', None, 'dp'), may hold values from -0.09375 to 0.09375
- w_down: bfloat16 [8, 8192, 4096], P('expert', None, 'dp'), may hold values from -0.0625 to 0.0625
Outputs:
- mixed: bfloat16 [4096, 4096], P(('expert', 'dp'))
Inputs may be any that keep to these rules, and one draw needn't show every extreme that they name: `expert_ids`: each token names 2 different experts. Within each aligned block of 8 tokens (the tokens of one device), the assignments to one expert get distinct slots among 0 to 1 in some order, at most 2 of them are kept and the others get -1; an expert with 2 or more assignments in the block has all 2 slots used. No two assignments of one block share an expert and a slot. In every block some expert has all 2 slots used.
All inputs are finite; a program needn't handle non-finite values.
Results may differ from a plain program's by a relative error of at most 0.0085.
Values may be sent and summed in bfloat16 or wider, within the bound.
No kernel may reach another device: no remote copies, remote signals or barrier semaphores. Data moves between devices by JAX's collectives and lax.ppermute only.
A program may use at most 128 MiB of HBM per device.

v0:
```python
import jax
import jax.numpy as jnp
from jax import lax
from jax.sharding import PartitionSpec as P

CAP = 2


def shards(tokens, expert_ids, slots, mix_weights, w_gate, w_up, w_down):
    tok_rows, model_width = tokens.shape
    experts = lax.axis_size("expert")
    capacity = CAP
    slot_count = experts * capacity
    slot_ids = jnp.arange(slot_count, dtype=jnp.int32)
    slot_expert = slot_ids // capacity
    slot_index = slot_ids % capacity
    matches = (expert_ids[None, :, :] == slot_expert[:, None, None]) & (
        slots[None, :, :] == slot_index[:, None, None]
    )
    occupied = jnp.any(matches, axis=2)
    dispatch_table = occupied.astype(jnp.bfloat16)
    outgoing = jnp.dot(dispatch_table, tokens, preferred_element_type=jnp.float32).astype(
        jnp.bfloat16
    )
    arrived = lax.all_to_all(outgoing, "expert", split_axis=0, concat_axis=0, tiled=True)
    gate_w = w_gate[0]
    up_w = w_up[0]
    down_w = w_down[0]
    portion = lax.all_gather(arrived, "dp", axis=0, tiled=True)
    gate_part = jnp.dot(portion, gate_w, preferred_element_type=jnp.float32)
    up_part = jnp.dot(portion, up_w, preferred_element_type=jnp.float32)
    hidden = (jax.nn.silu(gate_part) * up_part).astype(jnp.bfloat16)
    summed = jnp.dot(
        lax.all_gather(hidden, "dp", axis=1, tiled=True), down_w, preferred_element_type=jnp.float32
    )
    result = summed.astype(jnp.bfloat16)
    groups = lax.axis_size("dp")
    blocks = result.reshape(groups, experts, capacity, result.shape[1])
    blocks = lax.all_to_all(blocks, "expert", split_axis=1, concat_axis=1, tiled=True)
    blocks = lax.all_to_all(blocks, "dp", split_axis=0, concat_axis=3, tiled=True)
    returned = blocks.reshape(slot_count, model_width)
    weight_table = jnp.sum(jnp.where(matches, mix_weights[None, :, :], 0.0), axis=2)
    mixed = jnp.dot(
        weight_table.T, returned.astype(jnp.float32), preferred_element_type=jnp.float32
    )
    return mixed.astype(jnp.bfloat16)


def solution(mesh):
    placed = (
        P(("expert", "dp"), None),
        P(("expert", "dp"), None),
        P(("expert", "dp"), None),
        P(("expert", "dp"), None),
        P("expert", None, "dp"),
        P("expert", None, "dp"),
        P("expert", None, "dp"),
    )
    return jax.shard_map(
        shards, mesh=mesh, in_specs=placed, out_specs=P(("expert", "dp"), None), check_vma=False
    )
```

profile of v0, /device:TPU:1, one launch (start us, length us, event | category | flops | bytes accessed | tf_op | source)
XLA Modules:
  0.0 327.1 jit_solution(15211576409830812576)
XLA Ops:
  6.5 0.9 fusion.5
  7.5 1.1 convolution_convert_fusion
  8.5 0.1 all_to_all.22
  8.6 14.5 %all_to_all.32 = bf16[8,2,4096]{2,1,0:T(2,128)(2,1)S(1)} all-to-all(bf16[8,2,4096]{2,1,0:T(2,128)(2,1)S(1)} %all_to_all.22), channel_id=1, replica_groups=mesh['expert'=8,'dp'=64] {'expert'}, dimensions={0} | all-to-all | bytes 262144 | tf_op jit(solution)/shard_map/all_to_all | solution.py:25
  23.1 0.7 all_to_all.24
  23.8 0.0 all-gather.3.cloned.1.call-update
  23.8 0.0 all-gather.5.cloned.1.call-start
  23.9 98.3 %all-gather.3.cloned.1.call-done = bf16[1024,4096]{1,0:T(8,128)(2,1)} async-done(((bf16[16,4096]{1,0:T(8,128)(2,1)}), bf16[1024,4096]{1,0:T(8,128)(2,1)}) %all-gather.3.cloned.1.call-update) | async-done | bytes 8388624 | tf_op jit(solution)/shard_map/all_gather | solution.py:29
  122.2 5.8 %fusion.3 = f32[1024,128]{1,0:T(8,128)S(1)} fusion(bf16[1024,4096]{1,0:T(8,128)(2,1)} %all-gather.3.cloned.1.call-done, bf16[1,4096,128]{2,1,0:T(8,128)(2,1)S(1)} %copy-done), kind=kOutput, calls=%fused_computation.7 | convolution fusion | flops 1073741824 | bytes 9961472 | tf_op jit(solution)/shard_map/dot_general | solution.py:30
  128.1 0.0 copy-done.6
  128.1 0.0 copy-start.1
  128.1 3.0 fusion
  131.1 0.0 all-gather.5.cloned.1.call-update
  131.2 0.0 copy-start.2
  131.2 0.0 copy-start.3
  131.2 0.0 copy-start.4
  131.2 141.9 %all-gather.5.cloned.1.call-done = bf16[1024,8192]{1,0:T(8,128)(2,1)} async-done(((bf16[1024,128]{1,0:T(8,128)(2,1)}), bf16[1024,8192]{1,0:T(8,128)(2,1)}) %all-gather.5.cloned.1.call-update) | async-done | bytes 16777232 | tf_op jit(solution)/shard_map/all_gather | solution.py:34
  273.1 10.9 %convolution_convert_fusion.2 = bf16[1024,64]{0,1:T(8,128)(2,1)S(1)} fusion(bf16[1024,8192]{1,0:T(8,128)(2,1)} %all-gather.5.cloned.1.call-done, bf16[1,8192,64]{1,2,0:T(8,128)(2,1)S(1)} %copy-done.1), kind=kOutput, calls=%fused_computation.4 | convolution fusion | flops 1073807360 | bytes 17956864 | tf_op jit(solution)/shard_map/dot_general | solution.py:33
  284.1 0.2 copy.29
  284.3 0.2 copy.34
  284.4 0.2 reshape.36
  284.7 13.9 %all_to_all.33 = bf16[8,2,4096]{2,1,0:T(2,128)(2,1)S(1)} all-to-all(bf16[8,2,4096]{2,1,0:T(2,128)(2,1)S(1)} %reshape.36), channel_id=1, replica_groups=mesh['expert'=8,'dp'=64] {'expert'}, dimensions={0} | all-to-all | bytes 262144 | tf_op jit(solution)/shard_map/all_to_all | solution.py:39
  298.6 0.2 reshape.37
  298.9 0.2 copy.31
  299.0 0.8 reshape.38
  299.9 7.4 %all-to-all-start.2 = ((bf16[64,2,512]{2,1,0:T(2,128)(2,1)}), bf16[64,2,512]{2,1,0:T(2,128)(2,1)S(1)}, u32[]{:S(2)}, u32[]{:S(2)}) async-start(bf16[64,2,512]{2,1,0:T(2,128)(2,1)} %reshape.38), calls=%async_computation.2 | async-start | bytes 262144 | tf_op jit(solution)/shard_map/all_to_all | solution.py:40
  307.3 0.1 select_reduce_fusion
  307.4 11.5 %all-to-all-done.2 = bf16[64,2,512]{2,1,0:T(2,128)(2,1)S(1)} async-done(((bf16[64,2,512]{2,1,0:T(2,128)(2,1)}), bf16[64,2,512]{2,1,0:T(2,128)(2,1)S(1)}, u32[]{:S(2)}, u32[]{:S(2)}) %all-to-all-start.2) | async-done | bytes 131104 | tf_op jit(solution)/shard_map/all_to_all | solution.py:40
  318.9 0.2 reshape.39
  319.1 0.1 copy.32
  319.2 0.3 reshape.35
  319.4 0.8 fusion.6
  (11 shorter events, 0.0 us)
Async XLA Ops:
  6.5 115.7 %copy-start = (bf16[1,4096,128]{2,1,0:T(8,128)(2,1)S(1)}, bf16[1,4096,128]{2,1,0:T(8,128)(2,1)}, u32[]{:S(2)}) copy-start(bf16[1,4096,128]{2,1,0:T(8,128)(2,1)} %param.11) | copy-start | bytes 3145732
  6.5 121.5 %copy-start.6 = (bf16[1,4096,128]{2,1,0:T(8,128)(2,1)S(1)}, bf16[1,4096,128]{2,1,0:T(8,128)(2,1)}, u32[]{:S(2)}) copy-start(bf16[1,4096,128]{2,1,0:T(8,128)(2,1)} %param.12) | copy-start | bytes 3145732
  6.5 115.7 %all-gather.3.cloned.1.call-start = ((), (), s32[]{:S(2)}) async-start(), calls=%async_computation.3 | async-start | bytes 8519680 | tf_op jit(solution)/shard_map/all_gather | solution.py:29
  23.8 249.3 %all-gather.5.cloned.1.call-start = ((), (), s32[]{:S(2)}) async-start(), calls=%async_computation.4 | async-start | bytes 17039360 | tf_op jit(solution)/shard_map/all_gather | solution.py:34
  122.2 5.9 %copy-start.5 = (bf16[1024,4096]{1,0:T(8,128)(2,1)S(1)}, bf16[1024,4096]{1,0:T(8,128)(2,1)}, u32[]{:S(2)}) copy-start(bf16[1024,4096]{1,0:T(8,128)(2,1)} %all-gather.3.cloned.1.call-done) | copy-start | bytes 25165828
  128.1 145.1 %copy-start.1 = (bf16[1,8192,64]{1,2,0:T(8,128)(2,1)S(1)}, bf16[1,8192,64]{1,2,0:T(8,128)(2,1)}, u32[]{:S(2)}) copy-start(bf16[1,8192,64]{1,2,0:T(8,128)(2,1)} %param.13) | copy-start | bytes 3145732
  131.2 176.1 %copy-start.2 = (s32[8,2]{0,1:T(2,128)S(1)}, s32[8,2]{0,1:T(2,128)}, u32[]{:S(2)}) copy-start(s32[8,2]{0,1:T(2,128)} %param.9) | copy-start | bytes 196
  131.2 176.1 %copy-start.3 = (s32[8,2]{0,1:T(2,128)S(1)}, s32[8,2]{0,1:T(2,128)}, u32[]{:S(2)}) copy-start(s32[8,2]{0,1:T(2,128)} %param.8) | copy-start | bytes 196
  131.2 176.1 %copy-start.4 = (f32[8,2]{0,1:T(2,128)S(1)}, f32[8,2]{0,1:T(2,128)}, u32[]{:S(2)}) copy-start(f32[8,2]{0,1:T(2,128)} %param.10) | copy-start | bytes 196
  299.9 19.0 %all-to-all-start.2 = ((bf16[64,2,512]{2,1,0:T(2,128)(2,1)}), bf16[64,2,512]{2,1,0:T(2,128)(2,1)S(1)}, u32[]{:S(2)}, u32[]{:S(2)}) async-start(bf16[64,2,512]{2,1,0:T(2,128)(2,1)} %reshape.38), calls=%async_computation.2 | async-start | bytes 262144 | tf_op jit(solution)/shard_map/all_to_all | solution.py:40
Sparse Core Ops, SparseCore 0:
  24.0 98.1 all-gather.2
  131.3 141.7 all-gather.4
where the time goes:
time: 327 us
  waiting for transfers between devices  252 us (77%)
  blocking collectives  28.4 us (9%)
  matrix products  21.7 us (7%)
  between operations  13.6 us (4%)
  starting transfers between devices  7.4 us (2%)
    all_gather x1, waiting for transfers between devices, shards(): lax.all_gather(hidden, 'dp', axis=1, tiled=True)  142 us
    all_gather x1, waiting for transfers between devices, shards(): portion = lax.all_gather(arrived, 'dp', axis=0, tiled=True)  98.3 us
    all_to_all x1, blocking collectives, shards(): lax.all_to_all(outgoing, 'expert', split_axis=0, concat_axis=0, tiled=True)  14.5 us
    all_to_all x1, blocking collectives, shards(): lax.all_to_all(blocks, 'expert', split_axis=1, concat_axis=1, tiled=True)  13.9 us
    all_to_all x1, waiting for transfers between devices, shards(): lax.all_to_all(blocks, 'dp', split_axis=0, concat_axis=3, tiled=True)  11.5 us
    dot_general x1, matrix products, shards(): jnp.dot(lax.all_gather(hidden, 'dp', axis=1, tiled=True), down_w, preferr...  10.9 us
    all_to_all x1, starting transfers between devices, shards(): lax.all_to_all(blocks, 'dp', split_axis=0, concat_axis=3, tiled=True)  7.36 us
  transfers between devices with their start and end apart: 3, of which 3 were waited for; matrix products, arithmetic and copies ran while one was open for 0% of the time, Pallas kernels for 0%

commit v1 on v0

--- a/solution.py
+++ b/solution.py
@@ -4,6 +4,12 @@
 from jax.sharding import PartitionSpec as P
 
 CAP = 2
+
+
+def gather_from_all(x, axis, dim):
+    size = lax.axis_size(axis)
+    repeats = [size if d == dim else 1 for d in range(x.ndim)]
+    return lax.all_to_all(jnp.tile(x, repeats), axis, split_axis=dim, concat_axis=dim, tiled=True)
 
 
 def shards(tokens, expert_ids, slots, mix_weights, w_gate, w_up, w_down):
@@ -30,9 +36,7 @@
     gate_part = jnp.dot(portion, gate_w, preferred_element_type=jnp.float32)
     up_part = jnp.dot(portion, up_w, preferred_element_type=jnp.float32)
     hidden = (jax.nn.silu(gate_part) * up_part).astype(jnp.bfloat16)
-    summed = jnp.dot(
-        lax.all_gather(hidden, "dp", axis=1, tiled=True), down_w, preferred_element_type=jnp.float32
-    )
+    summed = jnp.dot(gather_from_all(hidden, "dp", 1), down_w, preferred_element_type=jnp.float32)
     result = summed.astype(jnp.bfloat16)
     groups = lax.axis_size("dp")
     blocks = result.reshape(groups, experts, capacity, result.shape[1])

time: 327 us -> 619 us (1.89)
  blocking collectives: 28.4 us -> 406 us
  waiting for transfers between devices: 252 us -> 110 us
  starting transfers between devices: 7.4 us -> 39.5 us
  local copies, waits for them, and re-layouts: 3.24 us -> 29.7 us
    all_to_all x0 -> x1, blocking collectives: none -> 380 us  [gather_from_all(): lax.all_to_all(jnp.tile(x, repeats), axis, split_axis=dim, concat_axis=di...]
    all_gather x1 -> x0, waiting for transfers between devices: 142 us -> none  [shards(): lax.all_gather(hidden, 'dp', axis=1, tiled=True)]
    all_to_all x1, starting transfers between devices: 7.36 us -> 39.5 us  [shards(): lax.all_to_all(blocks, 'dp', split_axis=0, concat_axis=3, tiled=True)]
    all_to_all x0 -> x1, local copies, waits for them, and re-layouts: none -> 22.4 us  [gather_from_all(): lax.all_to_all(jnp.tile(x, repeats), axis, split_axis=dim, concat_axis=di...]
  transfers between devices with their start and end apart: 3 -> 2, of which waited for: 3 -> 2; matrix products, arithmetic and copies ran while one was open for 0% -> 0% of each run, Pallas kernels for 0% -> 0%
where the time goes in v1:
time: 619 us; the launch traced here: 618 us
  blocking collectives  406 us (66%)
  waiting for transfers between devices  110 us (18%)
  starting transfers between devices  39.5 us (6%)
  local copies, waits for them, and re-layouts  29.7 us (5%)
  matrix products  18.9 us (3%)
  between operations  13.5 us (2%)
    all_to_all x1, blocking collectives, gather_from_all(): lax.all_to_all(jnp.tile(x, repeats), axis, split_axis=dim, concat_axis=di...  380 us
    all_gather x1, waiting for transfers between devices, shards(): portion = lax.all_gather(arrived, 'dp', axis=0, tiled=True)  98.3 us
    all_to_all x1, starting transfers between devices, shards(): lax.all_to_all(blocks, 'dp', split_axis=0, concat_axis=3, tiled=True)  39.5 us
    all_to_all x1, local copies, waits for them, and re-layouts, gather_from_all(): lax.all_to_all(jnp.tile(x, repeats), axis, split_axis=dim, concat_axis=di...  22.4 us
    all_to_all x1, blocking collectives, shards(): lax.all_to_all(outgoing, 'expert', split_axis=0, concat_axis=0, tiled=True)  14.5 us
  transfers between devices with their start and end apart: 2, of which 2 were waited for; matrix products, arithmetic and copies ran while one was open for 0% of the time, Pallas kernels for 0%

profile of v1, /device:TPU:1, one launch (start us, length us, event | category | flops | bytes accessed | tf_op | source)
XLA Modules:
  0.0 618.3 jit_solution(9586940807238596354)
XLA Ops:
  6.5 0.9 fusion.5
  7.5 1.1 convolution_convert_fusion
  8.5 0.1 all_to_all.28
  8.6 14.5 %all_to_all.41 = bf16[8,2,4096]{2,1,0:T(2,128)(2,1)S(1)} all-to-all(bf16[8,2,4096]{2,1,0:T(2,128)(2,1)S(1)} %all_to_all.28), channel_id=1, replica_groups=mesh['expert'=8,'dp'=64] {'expert'}, dimensions={0} | all-to-all | bytes 262144 | tf_op jit(solution)/shard_map/all_to_all | solution.py:31
  23.1 0.7 all_to_all.30
  23.8 0.0 all-gather.2.cloned.1.call-update
  23.8 98.3 %all-gather.2.cloned.1.call-done = bf16[1024,4096]{1,0:T(8,128)(2,1)} async-done(((bf16[16,4096]{1,0:T(8,128)(2,1)}), bf16[1024,4096]{1,0:T(8,128)(2,1)}) %all-gather.2.cloned.1.call-update) | async-done | bytes 8388624 | tf_op jit(solution)/shard_map/all_gather | solution.py:35
  122.2 0.0 copy-done
  122.2 5.9 fusion.3
  128.1 2.3 fusion
  130.4 4.1 tile.2
  134.5 379.7 %all_to_all.42 = bf16[1024,64,128]{2,0,1:T(8,128)(2,1)} all-to-all(bf16[1024,64,128]{2,0,1:T(8,128)(2,1)S(1)} %tile.2), channel_id=1, replica_groups=mesh['expert'=8,'dp'=64] {'dp'}, dimensions={1} | all-to-all | bytes 33554432 | tf_op jit(solution)/shard_map/all_to_all | solution.py:12
  514.2 22.4 %copy.37 = bf16[1024,64,128]{0,2,1:T(8,128)(2,1)} copy(bf16[1024,64,128]{2,0,1:T(8,128)(2,1)} %all_to_all.42) | data formatting | bytes 33554432 | tf_op jit(solution)/shard_map/all_to_all | solution.py:12
  536.7 0.0 copy-start.4
  536.7 8.9 %convolution_convert_fusion.2 = bf16[1024,64]{0,1:T(8,128)(2,1)S(1)} fusion(bf16[1024,8192]{0,1:T(8,128)(2,1)} %bitcast.27, bf16[1,8192,64]{1,2,0:T(8,128)(2,1)S(1)} %copy-done.1), kind=kOutput, calls=%fused_computation.4 | convolution fusion | flops 1073807360 | bytes 17956864 | tf_op jit(solution)/shard_map/dot_general | solution.py:39
  545.5 0.2 copy.38
  545.7 0.2 copy.43
  545.9 0.2 reshape.43
  546.1 11.6 %all_to_all.43 = bf16[8,2,4096]{2,1,0:T(2,128)(2,1)S(1)} all-to-all(bf16[8,2,4096]{2,1,0:T(2,128)(2,1)S(1)} %reshape.43), channel_id=1, replica_groups=mesh['expert'=8,'dp'=64] {'expert'}, dimensions={0} | all-to-all | bytes 262144 | tf_op jit(solution)/shard_map/all_to_all | solution.py:43
  557.7 0.2 reshape.44
  557.9 0.2 copy.40
  558.1 0.8 reshape.45
  559.0 39.5 %all-to-all-start.3 = ((bf16[64,2,512]{2,1,0:T(2,128)(2,1)}), bf16[64,2,512]{2,1,0:T(2,128)(2,1)S(1)}, u32[]{:S(2)}, u32[]{:S(2)}) async-start(bf16[64,2,512]{2,1,0:T(2,128)(2,1)} %reshape.45), calls=%async_computation.3 | async-start | bytes 262144 | tf_op jit(solution)/shard_map/all_to_all | solution.py:44
  598.5 0.0 copy-done.2
  598.5 0.0 copy-done.3
  598.5 0.0 copy-done.4
  598.5 0.1 select_reduce_fusion
  598.6 11.5 %all-to-all-done.3 = bf16[64,2,512]{2,1,0:T(2,128)(2,1)S(1)} async-done(((bf16[64,2,512]{2,1,0:T(2,128)(2,1)}), bf16[64,2,512]{2,1,0:T(2,128)(2,1)S(1)}, u32[]{:S(2)}, u32[]{:S(2)}) %all-to-all-start.3) | async-done | bytes 131104 | tf_op jit(solution)/shard_map/all_to_all | solution.py:44
  610.1 0.2 reshape.46
  610.3 0.1 copy.41
  610.4 0.3 reshape.42
  610.7 0.8 fusion.6
  (11 shorter events, 0.0 us)
Async XLA Ops:
  6.5 115.6 %copy-start = (bf16[1,4096,128]{2,1,0:T(8,128)(2,1)S(1)}, bf16[1,4096,128]{2,1,0:T(8,128)(2,1)}, u32[]{:S(2)}) copy-start(bf16[1,4096,128]{2,1,0:T(8,128)(2,1)} %param.11) | copy-start | bytes 3145732
  6.5 121.5 %copy-start.6 = (bf16[1,4096,128]{2,1,0:T(8,128)(2,1)S(1)}, bf16[1,4096,128]{2,1,0:T(8,128)(2,1)}, u32[]{:S(2)}) copy-start(bf16[1,4096,128]{2,1,0:T(8,128)(2,1)} %param.12) | copy-start | bytes 3145732
  6.5 115.6 %all-gather.2.cloned.1.call-start = ((), (), s32[]{:S(2)}) async-start(), calls=%async_computation.4 | async-start | bytes 8519680 | tf_op jit(solution)/shard_map/all_gather | solution.py:35
  122.2 5.9 copy-start.5
  514.2 22.4 %copy-start.1 = (bf16[1,8192,64]{1,2,0:T(8,128)(2,1)S(1)}, bf16[1,8192,64]{1,2,0:T(8,128)(2,1)}, u32[]{:S(2)}) copy-start(bf16[1,8192,64]{1,2,0:T(8,128)(2,1)} %param.13) | copy-start | bytes 3145732
  536.7 61.8 %copy-start.2 = (s32[8,2]{0,1:T(2,128)S(1)}, s32[8,2]{0,1:T(2,128)}, u32[]{:S(2)}) copy-start(s32[8,2]{0,1:T(2,128)} %param.9) | copy-start | bytes 196
  536.7 61.8 %copy-start.3 = (s32[8,2]{0,1:T(2,128)S(1)}, s32[8,2]{0,1:T(2,128)}, u32[]{:S(2)}) copy-start(s32[8,2]{0,1:T(2,128)} %param.8) | copy-start | bytes 196
  536.7 61.9 %copy-start.4 = (f32[8,2]{0,1:T(2,128)S(1)}, f32[8,2]{0,1:T(2,128)}, u32[]{:S(2)}) copy-start(f32[8,2]{0,1:T(2,128)} %param.10) | copy-start | bytes 196
  559.0 51.1 %all-to-all-start.3 = ((bf16[64,2,512]{2,1,0:T(2,128)(2,1)}), bf16[64,2,512]{2,1,0:T(2,128)(2,1)S(1)}, u32[]{:S(2)}, u32[]{:S(2)}) async-start(bf16[64,2,512]{2,1,0:T(2,128)(2,1)} %reshape.45), calls=%async_computation.3 | async-start | bytes 262144 | tf_op jit(solution)/shard_map/all_to_all | solution.py:44
Sparse Core Ops, SparseCore 0:
  23.9 98.1 all-gather.1
